TPU v7x, 32 devices: a whole 2x2x4 slice. The times are simulated.
32 devices in a mesh: clip: 2 (over x), tm: 16 (over z, y, core).
Axes of the slice: x: 2, y: 2, z: 4, core: 2. Of those that a mesh axis runs over, the one named last changes fastest.
Arguments:
- frames: bfloat16 [64, 1024, 256], P('tm', 'clip'), parts along dimension 1, may hold values from -6 to 6
- gain_one: float32 [256], replicated, may hold values from 0.25 to 1.75
- conv_one: bfloat16 [3, 3, 3, 256, 256], replicated, may hold values from -0.078125 to 0.078125
- gain_two: float32 [256], replicated, may hold values from 0.25 to 1.75
- conv_two: bfloat16 [3, 3, 3, 256, 256], replicated, may hold values from -0.078125 to 0.078125
- out_weight: bfloat16 [256, 256], replicated, may hold values from -0.375 to 0.375
Outputs:
- latent: bfloat16 [64, 1024, 256], P(None, ('clip', 'tm')), parts along dimension 1
There are 2 independent parts, one for each index of `clip`. A program takes and returns all parts, laid end to end along the dimension named above; an argument that names none is the same for every part. Nothing has to cross between parts.
All inputs are finite; a program needn't handle non-finite values.
Results may differ from a plain program's by a relative error of at most 0.0065.
Values may be sent and summed in bfloat16 or wider, within the bound.
A program may use at most 192 MiB of HBM per device.

v0:
```python
import jax
import jax.numpy as jnp
from jax import lax
from jax.sharding import PartitionSpec as P

ROWS = 4
COLS = 128


def passed_along(x, axis, by):
    size = lax.axis_size(axis)
    pairs = [(i, i + by) for i in range(size) if 0 <= i + by < size]
    return lax.ppermute(x, axis, pairs)


def norm_act(x, gain):
    values = x.astype(jnp.float32)
    scale = lax.rsqrt(jnp.mean(values * values, axis=-1, keepdims=True) + 1e-06)
    return jax.nn.silu(values * scale * gain).astype(jnp.bfloat16)


def causal_conv(act, kernel):
    extended = act.shape[0]
    outcount = extended - 2
    channels = act.shape[-1]
    grid = act.reshape(extended, ROWS, COLS, channels)
    padded = jnp.pad(grid, ((0, 0), (1, 1), (1, 1), (0, 0)))
    columns = jnp.concatenate(
        [
            padded[:, tap_r : tap_r + ROWS, tap_c : tap_c + COLS, :]
            for tap_r in range(3)
            for tap_c in range(3)
        ],
        axis=-1,
    )
    total = jnp.zeros((outcount * ROWS * COLS, channels), jnp.float32)
    for tap_t in range(3):
        window = columns[tap_t : tap_t + outcount].reshape(-1, 9 * channels)
        total = total + jnp.dot(
            window,
            kernel[tap_t].reshape(9 * channels, channels),
            preferred_element_type=jnp.float32,
        )
    return total.reshape(outcount, ROWS * COLS, channels)


def block_ext(extended, gain, kernel):
    act = norm_act(extended, gain)
    return (extended[2:].astype(jnp.float32) + causal_conv(act, kernel)).astype(jnp.bfloat16)


def with_previous(x):
    earlier = passed_along(x[-2:], "tm", 1)
    return jnp.concatenate([earlier, x], axis=0)


def body(frames, gain_one, conv_one, gain_two, conv_two, out_weight):
    channels = frames.shape[-1]
    local_frames = frames.shape[0]
    first = block_ext(with_previous(frames), gain_one, conv_one)
    source = with_previous(first)
    half = local_frames // 2
    received = []
    for index in range(2):
        part_out = block_ext(source[index * half : index * half + half + 2], gain_two, conv_two)
        result = jnp.dot(
            part_out.reshape(-1, channels), out_weight, preferred_element_type=jnp.float32
        )
        received.append(
            lax.all_to_all(
                result.reshape(part_out.shape).astype(jnp.bfloat16),
                "tm",
                split_axis=1,
                concat_axis=0,
                tiled=True,
            )
        )
    senders = received[0].shape[0] // half
    owned = received[0].shape[1]
    joined = jnp.concatenate(
        [piece.reshape(senders, half, owned, channels) for piece in received], axis=1
    )
    latent = joined.reshape(senders * local_frames, owned, channels)
    return latent


def solution(mesh):
    placed = (P("tm", "clip", None), P(), P(), P(), P(), P())
    return jax.shard_map(
        body, mesh=mesh, in_specs=placed, out_specs=P(None, ("clip", "tm"), None), check_vma=False
    )
```

profile of v0, /device:TPU:0, one launch (start us, length us, event | category | flops | bytes accessed | tf_op | source)
XLA Modules:
  0.0 102.8 jit_solution(9920365118946784368)
XLA Ops:
  0.0 1.1 %slice.138 = bf16[2,512,256]{2,1,0:T(8,128)(2,1)S(1)} slice(bf16[4,512,256]{2,1,0:T(8,128)(2,1)} %param.6), slice={[2:4], [0:512], [0:256]} | slice | bytes 1048576 | tf_op jit(solution)/shard_map/slice | solution.py:53
  1.1 2.6 %collective-permute-start = (bf16[2,512,256]{2,1,0:T(8,128)(2,1)S(1)}, bf16[2,512,256]{2,1,0:T(8,128)(2,1)S(1)}, u32[]{:S(2)}, u32[]{:S(2)}) collective-permute-start(bf16[2,512,256]{2,1,0:T(8,128)(2,1)S(1)} %slice.138), channel_id=1, source_target_pairs={{0,1},{1,2},{2,3},{3,4},{4,5},{5,6},{6,7},{7,8},{8,9},{9,10},{10,1... | collective-permute-start | bytes 1572872 | tf_op jit(solution)/shard_map/ppermute | solution.py:13
  3.7 3.7 %fusion.48 = (bf16[1,3,3,256,256]{4,3,2,1,0:T(8,128)(2,1)S(1)}, bf16[1,3,3,256,256]{4,3,2,1,0:T(8,128)(2,1)}, bf16[1,3,3,256,256]{4,3,2,1,0:T(8,128)(2,1)}) fusion(bf16[3,3,3,256,256]{4,3,2,1,0:T(8,128)(2,1)} %param.8), kind=kLoop, calls=%fused_computation.97 | loop fusion | bytes 7077888 | tf_op jit(solution)/shard_map/slice | solution.py:41
  7.9 1.1 %multiply_convert_fusion = bf16[6,4,128,256]{3,2,1,0:T(8,128)(2,1)S(1)} fusion(bf16[4,4,128,256]{3,2,1,0:T(8,128)(2,1)S(1)} %bitcast.70, bf16[2,4,128,256]{3,2,1,0:T(8,128)(2,1)S(1)} %bitcast.81, f32[256]{0:T(256)S(1)} %copy-done.12, f32[6,4,128]{2,1,0:T(4,128)S(1)} %rsqrt.28), kind=kLoop, calls=%fused_computation.8 | loop fusion | flops 7077888 | bytes 3159040 | tf_op jit(solution)/shard_map/convert_element_type | solution.py:19
  9.6 0.6 fusion.18
  10.1 0.8 fusion.19
  11.1 0.8 fusion.20
  12.6 0.6 fusion.23
  13.1 7.6 %fusion.44 = (bf16[4,4,128,2304]{3,2,1,0:T(8,128)(2,1)S(1)}, bf16[4,4,128,2304]{3,2,1,0:T(8,128)(2,1)}, bf16[4,4,128,2304]{3,2,1,0:T(8,128)(2,1)}) fusion(bf16[6,4,128,2304]{3,2,1,0:T(8,128)(2,1)S(1)} %fusion.23), kind=kLoop, calls=%fused_computation.93 | loop fusion | bytes 56623104 | tf_op jit(solution)/shard_map/slice | solution.py:38
  20.8 5.3 %fusion.49 = f32[2048,256]{1,0:T(8,128)S(1)} fusion(bf16[2048,2304]{1,0:T(8,128)(2,1)} %bitcast.73, bf16[2304,256]{1,0:T(8,128)(2,1)S(1)} %bitcast.92), kind=kOutput, calls=%fused_computation.98 | convolution fusion | flops 2415919104 | bytes 12713984 | tf_op jit(solution)/shard_map/dot_general | solution.py:39
  26.1 1.1 %copy-done.2 = bf16[4,4,128,2304]{3,2,1,0:T(8,128)(2,1)S(1)} copy-done((bf16[4,4,128,2304]{3,2,1,0:T(8,128)(2,1)S(1)}, bf16[4,4,128,2304]{3,2,1,0:T(8,128)(2,1)}, u32[]{:S(2)}) %copy-start.2) | copy-done | bytes 9437208
  27.5 2.8 %convolution_add_fusion.1 = f32[2048,256]{1,0:T(8,128)S(1)} fusion(f32[2048,256]{1,0:T(8,128)S(1)} %fusion.49, bf16[2048,2304]{1,0:T(8,128)(2,1)S(1)} %bitcast.72, bf16[2304,256]{1,0:T(8,128)(2,1)S(1)} %bitcast.91), kind=kOutput, calls=%fused_computation.15 | convolution fusion | flops 2416443392 | bytes 14811136 | tf_op jit(solution)/shard_map/dot_general | solution.py:39
  30.3 2.8 %convolution_add_fusion = f32[2048,256]{1,0:T(8,128)S(1)} fusion(f32[2048,256]{1,0:T(8,128)S(1)} %convolution_add_fusion.1, bf16[2048,2304]{1,0:T(8,128)(2,1)S(1)} %bitcast.71, bf16[2304,256]{1,0:T(8,128)(2,1)S(1)} %bitcast.90), kind=kOutput, calls=%fused_computation.14 | convolution fusion | flops 2416443392 | bytes 14811136 | tf_op jit(solution)/shard_map/dot_general | solution.py:39
  33.5 7.2 %collective-permute-start.1 = (bf16[2,512,256]{2,1,0:T(8,128)(2,1)S(1)}, bf16[2,512,256]{2,1,0:T(8,128)(2,1)S(1)}, u32[]{:S(2)}, u32[]{:S(2)}) collective-permute-start(bf16[2,512,256]{2,1,0:T(8,128)(2,1)S(1)} %slice.185), channel_id=1, source_target_pairs={{0,1},{1,2},{2,3},{3,4},{4,5},{5,6},{6,7},{7,8},{8,9},{9,10},{10,1... | collective-permute-start | bytes 1572872 | tf_op jit(solution)/shard_map/ppermute | solution.py:13
  41.0 1.0 collective-permute-done.1
  42.1 0.6 fusion
  42.7 1.4 %fusion.7 = (bf16[4,512,256]{2,1,0:T(8,128)(2,1)S(1)}, bf16[4,512,256]{2,1,0:T(8,128)(2,1)S(1)}) fusion(f32[256]{0:T(256)S(1)} %copy-done.13, f32[4,512]{1,0:T(4,128)S(1)} %get-tuple-element.25, bf16[4,512,256]{2,1,0:T(8,128)(2,1)S(1)} %add_convert_fusion, bf16[2,512,256]{2,1,0:T(8,128)(2,1)S(1)} %collective-permute-done.1, f32[4,512]{1,0:T(4,128)S(1)} %get-tuple-element.24), kind=kLoop, calls=%fused_computation.39 | loop fusion | flops 8912896 | bytes 3687424 | tf_op jit(solution)/shard_map/convert_element_type | solution.py:19
  46.0 1.4 %fusion.45 = (bf16[2,4,128,2304]{3,2,1,0:T(8,128)(2,1)S(1)}, bf16[2,4,128,2304]{3,2,1,0:T(8,128)(2,1)S(1)}, bf16[2,4,128,2304]{3,2,1,0:T(8,128)(2,1)S(1)}) fusion(bf16[4,4,128,2304]{3,2,1,0:T(8,128)(2,1)S(1)} %fusion.31), kind=kLoop, calls=%fused_computation.94 | loop fusion | bytes 28311552 | tf_op jit(solution)/shard_map/slice | solution.py:38
  47.5 1.4 %fusion.50 = f32[1024,256]{1,0:T(8,128)S(1)} fusion(bf16[1024,2304]{1,0:T(8,128)(2,1)S(1)} %bitcast.79, bf16[2304,256]{1,0:T(8,128)(2,1)S(1)} %bitcast.88), kind=kOutput, calls=%fused_computation.99 | convolution fusion | flops 1207959552 | bytes 6946816 | tf_op jit(solution)/shard_map/dot_general | solution.py:39
  48.9 1.4 %convolution_add_fusion.5 = f32[1024,256]{1,0:T(8,128)S(1)} fusion(f32[1024,256]{1,0:T(8,128)S(1)} %fusion.50, bf16[1024,2304]{1,0:T(8,128)(2,1)S(1)} %bitcast.77, bf16[2304,256]{1,0:T(8,128)(2,1)S(1)} %bitcast.86), kind=kOutput, calls=%fused_computation.60 | convolution fusion | flops 1208221696 | bytes 7995392 | tf_op jit(solution)/shard_map/dot_general | solution.py:39
  50.3 1.4 %convolution_add_fusion.4 = f32[1024,256]{1,0:T(8,128)S(1)} fusion(f32[1024,256]{1,0:T(8,128)S(1)} %convolution_add_fusion.5, bf16[1024,2304]{1,0:T(8,128)(2,1)S(1)} %bitcast.75, bf16[2304,256]{1,0:T(8,128)(2,1)S(1)} %bitcast.84), kind=kOutput, calls=%fused_computation.59 | convolution fusion | flops 1208221696 | bytes 7995392 | tf_op jit(solution)/shard_map/dot_general | solution.py:39
  52.0 1.3 %copy.8 = bf16[2,512,256]{2,0,1:T(2,128)(2,1)} copy(bf16[2,512,256]{2,1,0:T(8,128)(2,1)S(1)} %convolution_convert_fusion.1) | data formatting | bytes 1048576 | tf_op jit(solution)/shard_map/convert_element_type | solution.py:71
  53.3 14.7 %all-to-all-start = ((bf16[2,512,256]{2,0,1:T(2,128)(2,1)}), bf16[2,512,256]{2,0,1:T(2,128)(2,1)S(1)}, u32[]{:S(2)}, u32[]{:S(2)}) async-start(bf16[2,512,256]{2,0,1:T(2,128)(2,1)} %copy.8), calls=%async_computation | async-start | bytes 1048576 | tf_op jit(solution)/shard_map/all_to_all | solution.py:70
  69.9 1.4 %fusion.46 = (bf16[2,4,128,2304]{3,2,1,0:T(8,128)(2,1)S(1)}, bf16[2,4,128,2304]{3,2,1,0:T(8,128)(2,1)S(1)}, bf16[2,4,128,2304]{3,2,1,0:T(8,128)(2,1)S(1)}) fusion(bf16[4,4,128,2304]{3,2,1,0:T(8,128)(2,1)S(1)} %fusion.39), kind=kLoop, calls=%fused_computation.95 | loop fusion | bytes 28311552 | tf_op jit(solution)/shard_map/slice | solution.py:38
  71.4 1.4 %fusion.51 = f32[1024,256]{1,0:T(8,128)S(1)} fusion(bf16[1024,2304]{1,0:T(8,128)(2,1)S(1)} %bitcast.78, bf16[2304,256]{1,0:T(8,128)(2,1)S(1)} %bitcast.89), kind=kOutput, calls=%fused_computation.100 | convolution fusion | flops 1207959552 | bytes 6946816 | tf_op jit(solution)/shard_map/dot_general | solution.py:39
  72.8 1.4 %convolution_add_fusion.3 = f32[1024,256]{1,0:T(8,128)S(1)} fusion(f32[1024,256]{1,0:T(8,128)S(1)} %fusion.51, bf16[1024,2304]{1,0:T(8,128)(2,1)S(1)} %bitcast.76, bf16[2304,256]{1,0:T(8,128)(2,1)S(1)} %bitcast.87), kind=kOutput, calls=%fused_computation.58 | convolution fusion | flops 1208221696 | bytes 7995392 | tf_op jit(solution)/shard_map/dot_general | solution.py:39
  74.2 1.4 %convolution_add_fusion.2 = f32[1024,256]{1,0:T(8,128)S(1)} fusion(f32[1024,256]{1,0:T(8,128)S(1)} %convolution_add_fusion.3, bf16[1024,2304]{1,0:T(8,128)(2,1)S(1)} %bitcast.74, bf16[2304,256]{1,0:T(8,128)(2,1)S(1)} %bitcast.85), kind=kOutput, calls=%fused_computation.57 | convolution fusion | flops 1208221696 | bytes 7995392 | tf_op jit(solution)/shard_map/dot_general | solution.py:39
  75.9 0.5 copy.9
  76.4 5.9 %all-to-all-done = bf16[2,512,256]{2,0,1:T(2,128)(2,1)S(1)} async-done(((bf16[2,512,256]{2,0,1:T(2,128)(2,1)}), bf16[2,512,256]{2,0,1:T(2,128)(2,1)S(1)}, u32[]{:S(2)}, u32[]{:S(2)}) %all-to-all-start) | async-done | bytes 524320 | tf_op jit(solution)/shard_map/all_to_all | solution.py:70
  82.3 18.2 %all_to_all.30 = bf16[2,512,256]{2,0,1:T(2,128)(2,1)S(1)} all-to-all(bf16[2,512,256]{2,0,1:T(2,128)(2,1)S(1)} %copy.9), channel_id=1, replica_groups=mesh['clip'=2,'tm'=16] {'tm'}, dimensions={1} | all-to-all | bytes 1048576 | tf_op jit(solution)/shard_map/all_to_all | solution.py:70
  100.5 1.1 %pad_maximum_fusion.1 = bf16[16,4,32,256]{3,1,2,0:T(4,128)(2,1)S(1)} fusion(bf16[16,2,32,256]{3,1,2,0:T(2,128)(2,1)S(1)} %bitcast.83, bf16[16,2,32,256]{3,1,2,0:T(2,128)(2,1)S(1)} %bitcast.82), kind=kLoop, calls=%fused_computation.80 | loop fusion | flops 2097152 | bytes 2097152 | tf_op jit(solution)/shard_map/concatenate | solution.py:80
  101.6 1.2 %copy.10 = bf16[16,4,32,256]{3,2,1,0:T(8,128)(2,1)} copy(bf16[16,4,32,256]{3,1,2,0:T(4,128)(2,1)S(1)} %pad_maximum_fusion.1) | data formatting | bytes 2097152 | tf_op jit(solution)/shard_map/concatenate | solution.py:80
  (60 shorter events, 7.0 us)
Async XLA Ops:
  0.0 51.7 %copy-start = (bf16[256,256]{1,0:T(8,128)(2,1)S(1)}, bf16[256,256]{1,0:T(8,128)(2,1)}, u32[]{:S(2)}) copy-start(bf16[256,256]{1,0:T(8,128)(2,1)} %param.11) | copy-start | bytes 393220
  1.1 6.3 %copy-start.1 = (bf16[4,512,256]{2,1,0:T(8,128)(2,1)S(1)}, bf16[4,512,256]{2,1,0:T(8,128)(2,1)}, u32[]{:S(2)}) copy-start(bf16[4,512,256]{2,1,0:T(8,128)(2,1)} %param.6) | copy-start | bytes 3145732
  1.1 6.8 %copy-start.12 = (f32[256]{0:T(256)S(1)}, f32[256]{0:T(256)}, u32[]{:S(2)}) copy-start(f32[256]{0:T(256)} %param.7) | copy-start | bytes 3076
  1.1 6.3 %collective-permute-start = (bf16[2,512,256]{2,1,0:T(8,128)(2,1)S(1)}, bf16[2,512,256]{2,1,0:T(8,128)(2,1)S(1)}, u32[]{:S(2)}, u32[]{:S(2)}) collective-permute-start(bf16[2,512,256]{2,1,0:T(8,128)(2,1)S(1)} %slice.138), channel_id=1, source_target_pairs={{0,1},{1,2},{2,3},{3,4},{4,5},{5,6},{6,7},{7,8},{8,9},{9,10},{10,1... | collective-permute-start | bytes 1572872 | tf_op jit(solution)/shard_map/ppermute | solution.py:13
  13.1 7.6 %copy-start.11 = (bf16[1,3,3,256,256]{4,3,2,1,0:T(8,128)(2,1)S(1)}, bf16[1,3,3,256,256]{4,3,2,1,0:T(8,128)(2,1)}, u32[]{:S(2)}) copy-start(bf16[1,3,3,256,256]{4,3,2,1,0:T(8,128)(2,1)} %get-tuple-element.20) | copy-start | bytes 3538948
  20.8 6.4 %copy-start.2 = (bf16[4,4,128,2304]{3,2,1,0:T(8,128)(2,1)S(1)}, bf16[4,4,128,2304]{3,2,1,0:T(8,128)(2,1)}, u32[]{:S(2)}) copy-start(bf16[4,4,128,2304]{3,2,1,0:T(8,128)(2,1)} %get-tuple-element.8) | copy-start | bytes 28311556
  20.8 6.7 %copy-start.10 = (bf16[1,3,3,256,256]{4,3,2,1,0:T(8,128)(2,1)S(1)}, bf16[1,3,3,256,256]{4,3,2,1,0:T(8,128)(2,1)}, u32[]{:S(2)}) copy-start(bf16[1,3,3,256,256]{4,3,2,1,0:T(8,128)(2,1)} %get-tuple-element.21) | copy-start | bytes 3538948
  33.1 7.7 %copy-start.3 = (bf16[3,3,3,256,256]{4,3,2,1,0:T(8,128)(2,1)S(1)}, bf16[3,3,3,256,256]{4,3,2,1,0:T(8,128)(2,1)}, u32[]{:S(2)}) copy-start(bf16[3,3,3,256,256]{4,3,2,1,0:T(8,128)(2,1)} %param.10) | copy-start | bytes 10616836
  33.5 9.2 %copy-start.13 = (f32[256]{0:T(256)S(1)}, f32[256]{0:T(256)}, u32[]{:S(2)}) copy-start(f32[256]{0:T(256)} %param.9) | copy-start | bytes 3076
  33.5 8.6 %collective-permute-start.1 = (bf16[2,512,256]{2,1,0:T(8,128)(2,1)S(1)}, bf16[2,512,256]{2,1,0:T(8,128)(2,1)S(1)}, u32[]{:S(2)}, u32[]{:S(2)}) collective-permute-start(bf16[2,512,256]{2,1,0:T(8,128)(2,1)S(1)} %slice.185), channel_id=1, source_target_pairs={{0,1},{1,2},{2,3},{3,4},{4,5},{5,6},{6,7},{7,8},{8,9},{9,10},{10,1... | collective-permute-start | bytes 1572872 | tf_op jit(solution)/shard_map/ppermute | solution.py:13
  41.0 6.4 %copy-start.8 = (bf16[1,3,3,256,256]{4,3,2,1,0:T(8,128)(2,1)}, bf16[1,3,3,256,256]{4,3,2,1,0:T(8,128)(2,1)S(1)}, u32[]{:S(2)}) copy-start(bf16[1,3,3,256,256]{4,3,2,1,0:T(8,128)(2,1)S(1)} %get-tuple-element.17) | copy-start | bytes 3538948
  41.0 7.8 %copy-start.6 = (bf16[1,3,3,256,256]{4,3,2,1,0:T(8,128)(2,1)}, bf16[1,3,3,256,256]{4,3,2,1,0:T(8,128)(2,1)S(1)}, u32[]{:S(2)}) copy-start(bf16[1,3,3,256,256]{4,3,2,1,0:T(8,128)(2,1)S(1)} %get-tuple-element.18) | copy-start | bytes 3538948
  41.0 9.2 %copy-start.4 = (bf16[1,3,3,256,256]{4,3,2,1,0:T(8,128)(2,1)}, bf16[1,3,3,256,256]{4,3,2,1,0:T(8,128)(2,1)S(1)}, u32[]{:S(2)}) copy-start(bf16[1,3,3,256,256]{4,3,2,1,0:T(8,128)(2,1)S(1)} %get-tuple-element.16) | copy-start | bytes 3538948
  53.3 29.0 %all-to-all-start = ((bf16[2,512,256]{2,0,1:T(2,128)(2,1)}), bf16[2,512,256]{2,0,1:T(2,128)(2,1)S(1)}, u32[]{:S(2)}, u32[]{:S(2)}) async-start(bf16[2,512,256]{2,0,1:T(2,128)(2,1)} %copy.8), calls=%async_computation | async-start | bytes 1048576 | tf_op jit(solution)/shard_map/all_to_all | solution.py:70
  69.9 1.5 %copy-start.9 = (bf16[1,3,3,256,256]{4,3,2,1,0:T(8,128)(2,1)S(1)}, bf16[1,3,3,256,256]{4,3,2,1,0:T(8,128)(2,1)}, u32[]{:S(2)}) copy-start(bf16[1,3,3,256,256]{4,3,2,1,0:T(8,128)(2,1)} %copy-done.8) | copy-start | bytes 3538948
  71.4 1.4 %copy-start.7 = (bf16[1,3,3,256,256]{4,3,2,1,0:T(8,128)(2,1)S(1)}, bf16[1,3,3,256,256]{4,3,2,1,0:T(8,128)(2,1)}, u32[]{:S(2)}) copy-start(bf16[1,3,3,256,256]{4,3,2,1,0:T(8,128)(2,1)} %copy-done.6) | copy-start | bytes 3538948
  72.8 1.4 %copy-start.5 = (bf16[1,3,3,256,256]{4,3,2,1,0:T(8,128)(2,1)S(1)}, bf16[1,3,3,256,256]{4,3,2,1,0:T(8,128)(2,1)}, u32[]{:S(2)}) copy-start(bf16[1,3,3,256,256]{4,3,2,1,0:T(8,128)(2,1)} %copy-done.4) | copy-start | bytes 3538948
where the time goes:
time: 103 us
  local copies, waits for them, and re-layouts  27.7 us (27%)
  starting transfers between devices  24.5 us (24%)
  matrix products  19.8 us (19%)
  blocking collectives  18.2 us (18%)
  waiting for transfers between devices  6.88 us (7%)
  other arithmetic  5.04 us (5%)
    dot_general x9, matrix products, causal_conv(): jnp.dot(window, kernel[tap_t].reshape(9 * channels, channels), preferred_...  19.2 us
    all_to_all x1, blocking collectives, body(): lax.all_to_all(result.reshape(part_out.shape).astype(jnp.bfloat16), 'tm',...  18.2 us
    all_to_all x1, starting transfers between devices, body(): lax.all_to_all(result.reshape(part_out.shape).astype(jnp.bfloat16), 'tm',...  14.7 us
    slice x3, local copies, waits for them, and re-layouts, causal_conv(): window = columns[tap_t:tap_t + outcount].reshape(-1, 9 * channels)  10.5 us
    ppermute x2, starting transfers between devices, passed_along(): return lax.ppermute(x, axis, pairs)  9.81 us
    unnamed x52, local copies, waits for them, and re-layouts  8.14 us
    all_to_all x1, waiting for transfers between devices, body(): lax.all_to_all(result.reshape(part_out.shape).astype(jnp.bfloat16), 'tm',...  5.85 us
    slice x2, local copies, waits for them, and re-layouts, causal_conv(): kernel[tap_t].reshape(9 * channels, channels)  3.92 us
  transfers between devices with their start and end apart: 3, of which 2 were waited for; matrix products, arithmetic and copies ran while one was open for 12% of the time, Pallas kernels for 0%

commit v1 on v0

v1 whole, which is shorter than its diff:
```python
import functools

import jax
import jax.numpy as jnp
from jax import lax
from jax.experimental import pallas as pl
from jax.experimental.pallas import tpu as pltpu
from jax.sharding import PartitionSpec as P

ROWS = 4
COLS = 128
MESH = pl.DeviceIdType.MESH


def norm_act(x, gain):
    values = x.astype(jnp.float32)
    scale = lax.rsqrt(jnp.mean(values * values, axis=-1, keepdims=True) + 1e-06)
    scaled = values * scale * gain
    return scaled * (0.5 * jnp.tanh(0.5 * scaled) + 0.5)


def store_shifted(acts, frame, row, act):
    channels = act.shape[-1]
    place = lax.broadcasted_iota(jnp.int32, act.shape, 0)
    before = jnp.where(place == 0, 0.0, pltpu.roll(act, 1, 0))
    after = jnp.where(place == COLS - 1, 0.0, pltpu.roll(act, COLS - 1, 0))
    acts[frame, row, :, :channels] = before.astype(jnp.bfloat16)
    acts[frame, row, :, channels : 2 * channels] = act.astype(jnp.bfloat16)
    acts[frame, row, :, 2 * channels :] = after.astype(jnp.bfloat16)


def conv_row(acts, kernel, frame, row):
    total = None
    for tap_t in range(3):
        for tap_r in range(3):
            source = row + tap_r - 1
            if 0 <= source < ROWS:
                window = acts[frame + tap_t : frame + tap_t + 2, source]
                part = jnp.dot(
                    window.reshape(2 * COLS, window.shape[-1]),
                    kernel[tap_t * 3 + tap_r],
                    preferred_element_type=jnp.float32,
                )
                total = part if total is None else total + part
    return total


def fused(
    n,
    frames_ref,
    gain_one,
    conv_one,
    gain_two,
    conv_two,
    out_weight,
    out_ref,
    frames,
    halo_one,
    halo_two,
    edge_two,
    kernel_one,
    kernel_two,
    acts_one,
    acts_two,
    first,
    result,
    load_sems,
    halo_send,
    halo_recv,
    edge_send,
    edge_recv,
    out_send,
    out_recv,
    own_sem,
):
    me = lax.axis_index("tm")
    count = frames.shape[0]
    channels = frames.shape[-1]
    owned = result.shape[2]
    per_row = COLS // owned
    earlier = me - 1
    later = me + 1

    loads = [
        pltpu.make_async_copy(frames_ref, frames, load_sems.at[0]),
        pltpu.make_async_copy(conv_one, kernel_one, load_sems.at[1]),
        pltpu.make_async_copy(conv_two, kernel_two, load_sems.at[2]),
    ]
    for load in loads:
        load.start()

    barrier = pltpu.get_barrier_semaphore()

    @pl.loop(1, n)
    def _(step):
        pl.semaphore_signal(
            barrier, inc=1, device_id={"tm": lax.rem(me + step, n)}, device_id_type=MESH
        )

    loads[0].wait()

    @pl.loop(0, count * ROWS)
    def _(index):
        frame = index // ROWS
        row = index % ROWS
        act = norm_act(frames[frame, row], gain_one[...])
        store_shifted(acts_one, frame + 2, row, act)

    pl.semaphore_wait(barrier, n - 1)

    halo_copy = pltpu.make_async_remote_copy(
        src_ref=frames_ref.at[pl.ds(count - 2, 2)],
        dst_ref=halo_one,
        send_sem=halo_send,
        recv_sem=halo_recv,
        device_id={"tm": lax.rem(later, n)},
        device_id_type=MESH,
    )

    def edge_copy(row):
        return pltpu.make_async_remote_copy(
            src_ref=edge_two.at[row],
            dst_ref=halo_two.at[row],
            send_sem=edge_send.at[row],
            recv_sem=edge_recv.at[row],
            device_id={"tm": lax.rem(later, n)},
            device_id_type=MESH,
        )

    @pl.when(later < n)
    def _():
        halo_copy.start()

    loads[1].wait()

    def first_pair(frame):
        for row in range(ROWS):
            conv = conv_row(acts_one, kernel_one, frame, row).reshape(2, COLS, channels)
            for at in range(2):
                value = (frames[frame + at, row].astype(jnp.float32) + conv[at]).astype(
                    jnp.bfloat16
                )
                first[frame + at, row] = value
                act = norm_act(value, gain_two[...])
                store_shifted(acts_two, frame + at + 2, row, act)
                if frame == count - 2:
                    edge_two[row, at] = act.astype(jnp.bfloat16)
            if frame == count - 2:

                @pl.when(later < n)
                def _():
                    edge_copy(row).start()

    def second_pair(frame):
        for row in range(ROWS):
            conv = conv_row(acts_two, kernel_two, frame, row).reshape(2, COLS, channels)
            value = (first[frame : frame + 2, row].astype(jnp.float32) + conv).astype(jnp.bfloat16)
            latent = jnp.dot(
                value.reshape(2 * COLS, channels),
                out_weight[...],
                preferred_element_type=jnp.float32,
            ).astype(jnp.bfloat16)
            for at in range(2):
                for index in range(per_row):
                    begin = at * COLS + index * owned
                    result[row * per_row + index, frame + at] = latent[begin : begin + owned]

            @pl.loop(0, per_row)
            def _(index):
                owner = row * per_row + index

                @pl.when(owner != me)
                def _():
                    pltpu.make_async_remote_copy(
                        src_ref=result.at[owner, pl.ds(frame, 2)],
                        dst_ref=out_ref.at[pl.ds(me * count + frame, 2)],
                        send_sem=out_send,
                        recv_sem=out_recv,
                        device_id={"tm": owner},
                        device_id_type=MESH,
                    ).start()

    for frame in reversed(range(2, count, 2)):
        first_pair(frame)

    @pl.when(me > 0)
    def _():
        halo_copy.wait_recv()

        @pl.loop(0, 2 * ROWS)
        def _(index):
            frame = index // ROWS
            row = index % ROWS
            act = norm_act(halo_one[frame, row], gain_one[...])
            store_shifted(acts_one, frame, row, act)

    @pl.when(me == 0)
    def _():
        @pl.loop(0, 2 * ROWS)
        def _(index):
            blank = jnp.zeros((COLS, acts_one.shape[-1]), jnp.bfloat16)
            acts_one[index // ROWS, index % ROWS] = blank
            acts_two[index // ROWS, index % ROWS] = blank

    first_pair(0)
    loads[2].wait()
    for frame in reversed(range(2, count, 2)):
        second_pair(frame)

    @pl.when(me > 0)
    def _():
        for row in range(ROWS):
            edge_copy(row).wait_recv()
            for at in range(2):
                store_shifted(acts_two, at, row, halo_two[row, at].astype(jnp.float32))

    second_pair(0)
    own = pltpu.make_async_copy(result.at[me], out_ref.at[pl.ds(me * count, count)], own_sem)
    own.start()

    @pl.when(later < n)
    def _():
        halo_copy.wait_send()
        for row in range(ROWS):
            edge_copy(row).wait_send()

    others = out_ref.at[pl.ds(0, (n - 1) * count)]
    sent = result.at[pl.ds(0, n - 1)]
    pltpu.make_async_copy(sent, sent, out_send).wait()
    pltpu.make_async_copy(others, others, out_recv).wait()
    own.wait()


def body(n, frames, gain_one, conv_one, gain_two, conv_two, out_weight):
    count, cells, channels = frames.shape
    owned = cells // n
    grid = (count, ROWS, COLS, channels)
    taps = (9, 3 * channels, channels)
    half = jnp.bfloat16
    hbm = pl.BlockSpec(memory_space=pl.ANY)
    vmem = pl.BlockSpec(memory_space=pltpu.VMEM)
    return pl.pallas_call(
        functools.partial(fused, n),
        out_shape=jax.ShapeDtypeStruct((n * count, owned, channels), half),
        in_specs=[hbm, vmem, hbm, vmem, hbm, vmem],
        out_specs=hbm,
        scratch_shapes=[
            pltpu.VMEM(grid, half),
            pltpu.VMEM((2, ROWS, COLS, channels), half),
            pltpu.VMEM((ROWS, 2, COLS, channels), half),
            pltpu.VMEM((ROWS, 2, COLS, channels), half),
            pltpu.VMEM(taps, half),
            pltpu.VMEM(taps, half),
            pltpu.VMEM((count + 2, ROWS, COLS, 3 * channels), half),
            pltpu.VMEM((count + 2, ROWS, COLS, 3 * channels), half),
            pltpu.VMEM(grid, half),
            pltpu.VMEM((n, count, owned, channels), half),
            pltpu.SemaphoreType.DMA((3,)),
            pltpu.SemaphoreType.DMA,
            pltpu.SemaphoreType.DMA,
            pltpu.SemaphoreType.DMA((ROWS,)),
            pltpu.SemaphoreType.DMA((ROWS,)),
            pltpu.SemaphoreType.DMA,
            pltpu.SemaphoreType.DMA,
            pltpu.SemaphoreType.DMA,
        ],
        compiler_params=pltpu.CompilerParams(collective_id=0, has_side_effects=True),
    )(
        frames.reshape(grid),
        gain_one.reshape(1, channels),
        conv_one.reshape(taps),
        gain_two.reshape(1, channels),
        conv_two.reshape(taps),
        out_weight,
    )


def solution(mesh):
    placed = (P("tm", "clip", None), P(), P(), P(), P(), P())
    return jax.shard_map(
        functools.partial(body, mesh.shape["tm"]),
        mesh=mesh,
        in_specs=placed,
        out_specs=P(None, ("clip", "tm"), None),
        check_vma=False,
    )
```

time: 103 us -> 48.6 us (0.47)
  the two profiles are of different devices: /device:TPU:0 before, /device:TPU:29 now
where the time goes in v1:
time: 48.6 us; the launch traced here: 48.5 us
  Pallas kernels  46.2 us (95%)
  local copies, waits for them, and re-layouts  2.26 us (5%)
    pallas_call x1, Pallas kernels, body(): pl.pallas_call(functools.partial(fused, n), out_shape=jax.ShapeDtypeStruc...  46.2 us
    unnamed x1, local copies, waits for them, and re-layouts  2.26 us

profile of v1, /device:TPU:29, one launch (start us, length us, event | category | flops | bytes accessed | tf_op | source)
XLA Modules:
  0.0 48.5 jit_solution(18438222059876003965)
XLA Ops:
  0.0 46.2 %shard_map.64 = bf16[64,32,256]{2,1,0:T(8,128)(2,1)} custom-call(bf16[4,4,128,256]{3,2,1,0:T(8,128)(2,1)} %bitcast.7, f32[1,256]{1,0:T(1,128)} %bitcast.8, bf16[9,768,256]{2,1,0:T(8,128)(2,1)} %bitcast.5, f32[1,256]{1,0:T(1,128)} %bitcast.9, bf16[9,768,256]{2,1,0:T(8,128)(2,1)} %bitcast.6, bf16[256,256]{1,0:T(8,128)(2,1)} %out_weight.1), custom_call_target="tpu_custom_call" | custom-call | tf_op jit(solution)/shard_map/pallas_call | solution.py:242
  46.2 2.3 %copy.8 = bf16[64,32,256]{2,1,0:T(8,128)(2,1)} copy(bf16[64,32,256]{2,1,0:T(8,128)(2,1)} %shard_map.64) | data formatting | bytes 2097152

commit v2 on v1

--- a/solution.py
+++ b/solution.py
@@ -29,20 +29,24 @@
     acts[frame, row, :, 2 * channels :] = after.astype(jnp.bfloat16)
 
 
-def conv_row(acts, kernel, frame, row):
+def conv_row(acts, kernel, frame, source, tap, rows):
     total = None
     for tap_t in range(3):
-        for tap_r in range(3):
-            source = row + tap_r - 1
-            if 0 <= source < ROWS:
-                window = acts[frame + tap_t : frame + tap_t + 2, source]
-                part = jnp.dot(
-                    window.reshape(2 * COLS, window.shape[-1]),
-                    kernel[tap_t * 3 + tap_r],
-                    preferred_element_type=jnp.float32,
-                )
-                total = part if total is None else total + part
-    return total
+        for at in range(rows):
+            window = acts[pl.ds(frame + tap_t, 2), source + at]
+            part = jnp.dot(
+                window.reshape(2 * COLS, window.shape[-1]),
+                kernel[tap_t * 3 + tap + at],
+                preferred_element_type=jnp.float32,
+            )
+            total = part if total is None else total + part
+    return total.reshape(2, COLS, total.shape[-1])
+
+
+def both_rows(acts, kernel, frame, half):
+    border = conv_row(acts, kernel, frame, 2 * half, 1 - half, 2)
+    inner = conv_row(acts, kernel, frame, half, 0, 3)
+    return (((ROWS - 1) * half, border), (1 + half, inner))
 
 
 def fused(
@@ -60,6 +64,7 @@
     edge_two,
     kernel_one,
     kernel_two,
+    project,
     acts_one,
     acts_two,
     first,
@@ -81,12 +86,13 @@
     earlier = me - 1
     later = me + 1
 
-    loads = [
-        pltpu.make_async_copy(frames_ref, frames, load_sems.at[0]),
-        pltpu.make_async_copy(conv_one, kernel_one, load_sems.at[1]),
-        pltpu.make_async_copy(conv_two, kernel_two, load_sems.at[2]),
-    ]
-    for load in loads:
+    loads = [pltpu.make_async_copy(frames_ref, frames, load_sems.at[0])]
+    for source, target in ((conv_one, kernel_one), (conv_two, kernel_two)):
+        for tap in range(9):
+            sem = load_sems.at[len(loads)]
+            loads.append(pltpu.make_async_copy(source.at[tap], target.at[tap], sem))
+    loads.append(pltpu.make_async_copy(out_weight, project, load_sems.at[19]))
+    for load in loads[:10]:
         load.start()
 
     barrier = pltpu.get_barrier_semaphore()
@@ -131,39 +137,81 @@
     def _():
         halo_copy.start()
 
-    loads[1].wait()
-
-    def first_pair(frame):
-        for row in range(ROWS):
-            conv = conv_row(acts_one, kernel_one, frame, row).reshape(2, COLS, channels)
+    for load in loads[1:10]:
+        load.wait()
+    for load in loads[10:]:
+        load.start()
+
+    halves = ROWS // 2
+    steps = (count // 2) * halves
+
+    @pl.loop(0, steps)
+    def _(step):
+        frame = count - 2 - 2 * (step // halves)
+        half = step % halves
+
+        @pl.when((step == steps - halves) & (me > 0))
+        def _():
+            halo_copy.wait_recv()
+
+            @pl.loop(0, 2 * ROWS)
+            def _(index):
+                at = index // ROWS
+                row = index % ROWS
+                store_shifted(acts_one, at, row, norm_act(halo_one[at, row], gain_one[...]))
+
+        @pl.when((step == steps - halves) & (me == 0))
+        def _():
+            @pl.loop(0, 2 * ROWS)
+            def _(index):
+                blank = jnp.zeros((COLS, acts_one.shape[-1]), jnp.bfloat16)
+                acts_one[index // ROWS, index % ROWS] = blank
+                acts_two[index // ROWS, index % ROWS] = blank
+
+        for row, conv in both_rows(acts_one, kernel_one, frame, half):
             for at in range(2):
                 value = (frames[frame + at, row].astype(jnp.float32) + conv[at]).astype(
                     jnp.bfloat16
                 )
                 first[frame + at, row] = value
-                act = norm_act(value, gain_two[...])
-                store_shifted(acts_two, frame + at + 2, row, act)
-                if frame == count - 2:
-                    edge_two[row, at] = act.astype(jnp.bfloat16)
-            if frame == count - 2:
-
-                @pl.when(later < n)
-                def _():
-                    edge_copy(row).start()
-
-    def second_pair(frame):
-        for row in range(ROWS):
-            conv = conv_row(acts_two, kernel_two, frame, row).reshape(2, COLS, channels)
-            value = (first[frame : frame + 2, row].astype(jnp.float32) + conv).astype(jnp.bfloat16)
+                store_shifted(acts_two, frame + at + 2, row, norm_act(value, gain_two[...]))
+
+        @pl.when((step < halves) & (later < n))
+        def _():
+            for row in ((ROWS - 1) * half, 1 + half):
+                for at in range(2):
+                    edge_two[row, at] = acts_two[count + at, row, :, channels : 2 * channels]
+                edge_copy(row).start()
+
+    for load in loads[10:]:
+        load.wait()
+
+    @pl.loop(0, steps)
+    def _(step):
+        frame = count - 2 - 2 * (step // halves)
+        half = step % halves
+
+        @pl.when((step == steps - halves) & (me > 0))
+        def _():
+            @pl.loop(0, ROWS)
+            def _(row):
+                edge_copy(row).wait_recv()
+                for at in range(2):
+                    store_shifted(acts_two, at, row, halo_two[row, at].astype(jnp.float32))
+
+        for row, conv in both_rows(acts_two, kernel_two, frame, half):
+            value = (first[pl.ds(frame, 2), row].astype(jnp.float32) + conv).astype(jnp.bfloat16)
             latent = jnp.dot(
                 value.reshape(2 * COLS, channels),
-                out_weight[...],
+                project[...],
                 preferred_element_type=jnp.float32,
             ).astype(jnp.bfloat16)
             for at in range(2):
                 for index in range(per_row):
                     begin = at * COLS + index * owned
                     result[row * per_row + index, frame + at] = latent[begin : begin + owned]
+
+        for row in ((ROWS - 1) * half, 1 + half):
 
             @pl.loop(0, per_row)
             def _(index):
@@ -180,41 +228,6 @@
                         device_id_type=MESH,
                     ).start()
 
-    for frame in reversed(range(2, count, 2)):
-        first_pair(frame)
-
-    @pl.when(me > 0)
-    def _():
-        halo_copy.wait_recv()
-
-        @pl.loop(0, 2 * ROWS)
-        def _(index):
-            frame = index // ROWS
-            row = index % ROWS
-            act = norm_act(halo_one[frame, row], gain_one[...])
-            store_shifted(acts_one, frame, row, act)
-
-    @pl.when(me == 0)
-    def _():
-        @pl.loop(0, 2 * ROWS)
-        def _(index):
-            blank = jnp.zeros((COLS, acts_one.shape[-1]), jnp.bfloat16)
-            acts_one[index // ROWS, index % ROWS] = blank
-            acts_two[index // ROWS, index % ROWS] = blank
-
-    first_pair(0)
-    loads[2].wait()
-    for frame in reversed(range(2, count, 2)):
-        second_pair(frame)
-
-    @pl.when(me > 0)
-    def _():
-        for row in range(ROWS):
-            edge_copy(row).wait_recv()
-            for at in range(2):
-                store_shifted(acts_two, at, row, halo_two[row, at].astype(jnp.float32))
-
-    second_pair(0)
     own = pltpu.make_async_copy(result.at[me], out_ref.at[pl.ds(me * count, count)], own_sem)
     own.start()
 
@@ -242,7 +255,7 @@
     return pl.pallas_call(
         functools.partial(fused, n),
         out_shape=jax.ShapeDtypeStruct((n * count, owned, channels), half),
-        in_specs=[hbm, vmem, hbm, vmem, hbm, vmem],
+        in_specs=[hbm, vmem, hbm, vmem, hbm, hbm],
         out_specs=hbm,
         scratch_shapes=[
             pltpu.VMEM(grid, half),
@@ -251,11 +264,12 @@
             pltpu.VMEM((ROWS, 2, COLS, channels), half),
             pltpu.VMEM(taps, half),
             pltpu.VMEM(taps, half),
+            pltpu.VMEM((channels, channels), half),
             pltpu.VMEM((count + 2, ROWS, COLS, 3 * channels), half),
             pltpu.VMEM((count + 2, ROWS, COLS, 3 * channels), half),
             pltpu.VMEM(grid, half),
             pltpu.VMEM((n, count, owned, channels), half),
-            pltpu.SemaphoreType.DMA((3,)),
+            pltpu.SemaphoreType.DMA((20,)),
             pltpu.SemaphoreType.DMA,
             pltpu.SemaphoreType.DMA,
             pltpu.SemaphoreType.DMA((ROWS,)),

time: 48.6 us -> 43.9 us (0.903)
  the two profiles are of different devices: /device:TPU:29 before, /device:TPU:21 now
where the time goes in v2:
time: 43.9 us; the launch traced here: 43.6 us
  Pallas kernels  41.3 us (94%)
  local copies, waits for them, and re-layouts  2.26 us (5%)
    pallas_call x1, Pallas kernels, body(): pl.pallas_call(functools.partial(fused, n), out_shape=jax.ShapeDtypeStruc...  41.3 us
    unnamed x1, local copies, waits for them, and re-layouts  2.26 us

profile of v2, /device:TPU:21, one launch (start us, length us, event | category | flops | bytes accessed | tf_op | source)
XLA Modules:
  0.0 43.6 jit_solution(12029828591840838780)
XLA Ops:
  0.0 41.3 %shard_map.64 = bf16[64,32,256]{2,1,0:T(8,128)(2,1)} custom-call(bf16[4,4,128,256]{3,2,1,0:T(8,128)(2,1)} %bitcast.7, f32[1,256]{1,0:T(1,128)} %bitcast.8, bf16[9,768,256]{2,1,0:T(8,128)(2,1)} %bitcast.5, f32[1,256]{1,0:T(1,128)} %bitcast.9, bf16[9,768,256]{2,1,0:T(8,128)(2,1)} %bitcast.6, bf16[256,256]{1,0:T(8,128)(2,1)} %out_weight.1), custom_call_target="tpu_custom_call" | custom-call | tf_op jit(solution)/shard_map/pallas_call | solution.py:255
  41.4 2.3 %copy.8 = bf16[64,32,256]{2,1,0:T(8,128)(2,1)} copy(bf16[64,32,256]{2,1,0:T(8,128)(2,1)} %shard_map.64) | data formatting | bytes 2097152

commit v3 on v2

--- a/solution.py
+++ b/solution.py
@@ -143,7 +143,9 @@
         load.start()
 
     halves = ROWS // 2
-    steps = (count // 2) * halves
+    pairs = count // 2
+    steps = pairs * halves
+    far = 1 - (2 * me) // n
 
     @pl.loop(0, steps)
     def _(step):
@@ -188,10 +190,10 @@
 
     @pl.loop(0, steps)
     def _(step):
-        frame = count - 2 - 2 * (step // halves)
-        half = step % halves
-
-        @pl.when((step == steps - halves) & (me > 0))
+        frame = count - 2 - 2 * (step % pairs)
+        half = (far + step // pairs) % halves
+
+        @pl.when((step == pairs - 1) & (me > 0))
         def _():
             @pl.loop(0, ROWS)
             def _(row):

time: 43.9 us -> 43.1 us (0.982)
  the two profiles are of different devices: /device:TPU:21 before, /device:TPU:11 now
where the time goes in v3:
time: 43.1 us; the launch traced here: 43 us
  Pallas kernels  40.7 us (94%)
  local copies, waits for them, and re-layouts  2.26 us (5%)
    pallas_call x1, Pallas kernels, body(): pl.pallas_call(functools.partial(fused, n), out_shape=jax.ShapeDtypeStruc...  40.7 us
    unnamed x1, local copies, waits for them, and re-layouts  2.26 us

profile of v3, /device:TPU:11, one launch (start us, length us, event | category | flops | bytes accessed | tf_op | source)
XLA Modules:
  0.0 43.0 jit_solution(127432218554854150)
XLA Ops:
  0.0 40.7 %shard_map.64 = bf16[64,32,256]{2,1,0:T(8,128)(2,1)} custom-call(bf16[4,4,128,256]{3,2,1,0:T(8,128)(2,1)} %bitcast.7, f32[1,256]{1,0:T(1,128)} %bitcast.8, bf16[9,768,256]{2,1,0:T(8,128)(2,1)} %bitcast.5, f32[1,256]{1,0:T(1,128)} %bitcast.9, bf16[9,768,256]{2,1,0:T(8,128)(2,1)} %bitcast.6, bf16[256,256]{1,0:T(8,128)(2,1)} %out_weight.1), custom_call_target="tpu_custom_call" | custom-call | tf_op jit(solution)/shard_map/pallas_call | solution.py:257
  40.7 2.3 %copy.8 = bf16[64,32,256]{2,1,0:T(8,128)(2,1)} copy(bf16[64,32,256]{2,1,0:T(8,128)(2,1)} %shard_map.64) | data formatting | bytes 2097152

commit v4 on v3

--- a/solution.py
+++ b/solution.py
@@ -144,76 +144,93 @@
 
     halves = ROWS // 2
     pairs = count // 2
-    steps = pairs * halves
     far = 1 - (2 * me) // n
 
-    @pl.loop(0, steps)
-    def _(step):
-        frame = count - 2 - 2 * (step // halves)
-        half = step % halves
-
-        @pl.when((step == steps - halves) & (me > 0))
+    def finish(frame, row, conv):
+        value = (first[pl.ds(frame, 2), row].astype(jnp.float32) + conv).astype(jnp.bfloat16)
+        latent = jnp.dot(
+            value.reshape(2 * COLS, channels),
+            project[...],
+            preferred_element_type=jnp.float32,
+        ).astype(jnp.bfloat16)
+        for at in range(2):
+            for index in range(per_row):
+                begin = at * COLS + index * owned
+                result[row * per_row + index, frame + at] = latent[begin : begin + owned]
+
+    @pl.loop(0, halves)
+    def _(stage):
+        near = (far + stage) % halves
+
+        @pl.loop(0, pairs)
+        def _(step):
+            frame = count - 2 - 2 * step
+            head = (stage == 0) & (step == pairs - 1)
+
+            @pl.when(head & (me > 0))
+            def _():
+                halo_copy.wait_recv()
+
+                @pl.loop(0, 2 * ROWS)
+                def _(index):
+                    at = index // ROWS
+                    row = index % ROWS
+                    store_shifted(acts_one, at, row, norm_act(halo_one[at, row], gain_one[...]))
+
+            @pl.when(head & (me == 0))
+            def _():
+                @pl.loop(0, 2 * ROWS)
+                def _(index):
+                    blank = jnp.zeros((COLS, acts_one.shape[-1]), jnp.bfloat16)
+                    acts_one[index // ROWS, index % ROWS] = blank
+                    acts_two[index // ROWS, index % ROWS] = blank
+
+            for row, conv in both_rows(acts_one, kernel_one, frame, near):
+                for at in range(2):
+                    value = (frames[frame + at, row].astype(jnp.float32) + conv[at]).astype(
+                        jnp.bfloat16
+                    )
+                    first[frame + at, row] = value
+                    store_shifted(acts_two, frame + at + 2, row, norm_act(value, gain_two[...]))
+
+            @pl.when((step == 0) & (later < n))
+            def _():
+                for row in ((ROWS - 1) * near, 1 + near):
+                    for at in range(2):
+                        edge_two[row, at] = acts_two[count + at, row, :, channels : 2 * channels]
+                    edge_copy(row).start()
+
+        @pl.when(stage == 0)
         def _():
-            halo_copy.wait_recv()
-
-            @pl.loop(0, 2 * ROWS)
-            def _(index):
-                at = index // ROWS
-                row = index % ROWS
-                store_shifted(acts_one, at, row, norm_act(halo_one[at, row], gain_one[...]))
-
-        @pl.when((step == steps - halves) & (me == 0))
-        def _():
-            @pl.loop(0, 2 * ROWS)
-            def _(index):
-                blank = jnp.zeros((COLS, acts_one.shape[-1]), jnp.bfloat16)
-                acts_one[index // ROWS, index % ROWS] = blank
-                acts_two[index // ROWS, index % ROWS] = blank
-
-        for row, conv in both_rows(acts_one, kernel_one, frame, half):
-            for at in range(2):
-                value = (frames[frame + at, row].astype(jnp.float32) + conv[at]).astype(
-                    jnp.bfloat16
-                )
-                first[frame + at, row] = value
-                store_shifted(acts_two, frame + at + 2, row, norm_act(value, gain_two[...]))
-
-        @pl.when((step < halves) & (later < n))
-        def _():
-            for row in ((ROWS - 1) * half, 1 + half):
-                for at in range(2):
-                    edge_two[row, at] = acts_two[count + at, row, :, channels : 2 * channels]
-                edge_copy(row).start()
-
-    for load in loads[10:]:
-        load.wait()
-
-    @pl.loop(0, steps)
-    def _(step):
-        frame = count - 2 - 2 * (step % pairs)
-        half = (far + step // pairs) % halves
-
-        @pl.when((step == pairs - 1) & (me > 0))
-        def _():
-            @pl.loop(0, ROWS)
-            def _(row):
-                edge_copy(row).wait_recv()
-                for at in range(2):
-                    store_shifted(acts_two, at, row, halo_two[row, at].astype(jnp.float32))
-
-        for row, conv in both_rows(acts_two, kernel_two, frame, half):
-            value = (first[pl.ds(frame, 2), row].astype(jnp.float32) + conv).astype(jnp.bfloat16)
-            latent = jnp.dot(
-                value.reshape(2 * COLS, channels),
-                project[...],
-                preferred_element_type=jnp.float32,
-            ).astype(jnp.bfloat16)
-            for at in range(2):
-                for index in range(per_row):
-                    begin = at * COLS + index * owned
-                    result[row * per_row + index, frame + at] = latent[begin : begin + owned]
-
-        for row in ((ROWS - 1) * half, 1 + half):
+            for load in loads[10:]:
+                load.wait()
+
+        @pl.loop(stage * pairs, (3 * stage + 1) * pairs)
+        def _(step):
+            unit = step // pairs
+            frame = count - 2 - 2 * (step % pairs)
+            half = (far + unit // 2) % halves
+            inner = unit % 2
+
+            @pl.when((unit < 2) & (frame == 0) & (me > 0))
+            def _():
+                @pl.loop(0, 2)
+                def _(index):
+                    row = 2 * near + index
+                    edge_copy(row).wait_recv()
+                    for at in range(2):
+                        store_shifted(acts_two, at, row, halo_two[row, at].astype(jnp.float32))
+
+            @pl.when(inner == 0)
+            def _():
+                conv = conv_row(acts_two, kernel_two, frame, 2 * half, 1 - half, 2)
+                finish(frame, (ROWS - 1) * half, conv)
+
+            @pl.when(inner == 1)
+            def _():
+                finish(frame, 1 + half, conv_row(acts_two, kernel_two, frame, half, 0, 3))
+
+            row = 2 * half + (half + inner) % 2
 
             @pl.loop(0, per_row)
             def _(index):

time: 43.1 us -> 55 us (1.28)
  the two profiles are of different devices: /device:TPU:11 before, /device:TPU:21 now
where the time goes in v4:
time: 55 us; the launch traced here: 54.8 us
  Pallas kernels  52.5 us (95%)
  local copies, waits for them, and re-layouts  2.26 us (4%)
    pallas_call x1, Pallas kernels, body(): pl.pallas_call(functools.partial(fused, n), out_shape=jax.ShapeDtypeStruc...  52.5 us
    unnamed x1, local copies, waits for them, and re-layouts  2.26 us

profile of v4, /device:TPU:21, one launch (start us, length us, event | category | flops | bytes accessed | tf_op | source)
XLA Modules:
  0.0 54.8 jit_solution(7522308395916571375)
XLA Ops:
  0.0 52.5 %shard_map.64 = bf16[64,32,256]{2,1,0:T(8,128)(2,1)} custom-call(bf16[4,4,128,256]{3,2,1,0:T(8,128)(2,1)} %bitcast.7, f32[1,256]{1,0:T(1,128)} %bitcast.8, bf16[9,768,256]{2,1,0:T(8,128)(2,1)} %bitcast.5, f32[1,256]{1,0:T(1,128)} %bitcast.9, bf16[9,768,256]{2,1,0:T(8,128)(2,1)} %bitcast.6, bf16[256,256]{1,0:T(8,128)(2,1)} %out_weight.1), custom_call_target="tpu_custom_call" | custom-call | tf_op jit(solution)/shard_map/pallas_call | solution.py:274
  52.5 2.3 %copy.8 = bf16[64,32,256]{2,1,0:T(8,128)(2,1)} copy(bf16[64,32,256]{2,1,0:T(8,128)(2,1)} %shard_map.64) | data formatting | bytes 2097152

commit v5 on v4

--- a/solution.py
+++ b/solution.py
@@ -144,6 +144,7 @@
 
     halves = ROWS // 2
     pairs = count // 2
+    steps = pairs * halves
     far = 1 - (2 * me) // n
 
     def finish(frame, row, conv):
@@ -160,12 +161,12 @@
 
     @pl.loop(0, halves)
     def _(stage):
-        near = (far + stage) % halves
-
-        @pl.loop(0, pairs)
+
+        @pl.loop(stage * (steps - 1), steps - 1 + stage)
         def _(step):
-            frame = count - 2 - 2 * step
-            head = (stage == 0) & (step == pairs - 1)
+            frame = count - 2 - 2 * (step // halves)
+            near = (far + step) % halves
+            head = step == steps - halves
 
             @pl.when(head & (me > 0))
             def _():
@@ -193,7 +194,7 @@
                     first[frame + at, row] = value
                     store_shifted(acts_two, frame + at + 2, row, norm_act(value, gain_two[...]))
 
-            @pl.when((step == 0) & (later < n))
+            @pl.when((step < halves) & (later < n))
             def _():
                 for row in ((ROWS - 1) * near, 1 + near):
                     for at in range(2):
@@ -212,11 +213,10 @@
             half = (far + unit // 2) % halves
             inner = unit % 2
 
-            @pl.when((unit < 2) & (frame == 0) & (me > 0))
-            def _():
-                @pl.loop(0, 2)
-                def _(index):
-                    row = 2 * near + index
+            @pl.when((step == pairs - 1) & (me > 0))
+            def _():
+                @pl.loop(0, ROWS)
+                def _(row):
                     edge_copy(row).wait_recv()
                     for at in range(2):
                         store_shifted(acts_two, at, row, halo_two[row, at].astype(jnp.float32))

time: 55 us -> 42.3 us (0.77)
  Pallas kernels: 52.5 us -> 39.9 us
    pallas_call x1, Pallas kernels: 52.5 us -> 39.9 us  [body(): pl.pallas_call(functools.partial(fused, n), out_shape=jax.ShapeDtypeStruc...]
where the time goes in v5:
time: 42.3 us; the launch traced here: 42.2 us
  Pallas kernels  39.9 us (94%)
  local copies, waits for them, and re-layouts  2.26 us (5%)
    pallas_call x1, Pallas kernels, body(): pl.pallas_call(functools.partial(fused, n), out_shape=jax.ShapeDtypeStruc...  39.9 us
    unnamed x1, local copies, waits for them, and re-layouts  2.26 us

profile of v5, /device:TPU:21, one launch (start us, length us, event | category | flops | bytes accessed | tf_op | source)
XLA Modules:
  0.0 42.2 jit_solution(9766874837494537816)
XLA Ops:
  0.0 39.9 %shard_map.64 = bf16[64,32,256]{2,1,0:T(8,128)(2,1)} custom-call(bf16[4,4,128,256]{3,2,1,0:T(8,128)(2,1)} %bitcast.7, f32[1,256]{1,0:T(1,128)} %bitcast.8, bf16[9,768,256]{2,1,0:T(8,128)(2,1)} %bitcast.5, f32[1,256]{1,0:T(1,128)} %bitcast.9, bf16[9,768,256]{2,1,0:T(8,128)(2,1)} %bitcast.6, bf16[256,256]{1,0:T(8,128)(2,1)} %out_weight.1), custom_call_target="tpu_custom_call" | custom-call | tf_op jit(solution)/shard_map/pallas_call | solution.py:274
  39.9 2.3 %copy.8 = bf16[64,32,256]{2,1,0:T(8,128)(2,1)} copy(bf16[64,32,256]{2,1,0:T(8,128)(2,1)} %shard_map.64) | data formatting | bytes 2097152
